TPU v7x, 32 devices: a whole 2x2x4 slice. The times are simulated.
32 devices in a mesh: table: 4 (over y, core), batch: 8 (over z, x).
Axes of the slice: x: 2, y: 2, z: 4, core: 2. Of those that a mesh axis runs over, the one named last changes fastest.
Arguments:
- emb: bfloat16 [4, 262144, 128], P('table', 'batch'), may hold values from -6 to 6
- short_rows: int32 [192, 4, 32], P(('table', 'batch')), may hold values from 0 to 262143
- short_len: int32 [192, 4], P(('table', 'batch')), may hold values from 1 to 32
- short_sample: int32 [192, 4], P(('table', 'batch')), may hold values from 0 to 7, as said below
- long_rows: int32 [64, 4, 512], P(('table', 'batch')), may hold values from 0 to 262143, as said below
- long_len: int32 [64, 4], P(('table', 'batch')), may hold values from 33 to 500, as said below
- long_sample: int32 [64, 4], P(('table', 'batch')), may hold values from 0 to 7, as said below
Outputs:
- pooled: float32 [256, 4, 128], P(('table', 'batch'))
Inputs may be any that keep to these rules, and one draw needn't show every extreme that they name: For each block of 6 short bags and 2 long bags with the same j // 6 and j // 2, and each table, short_sample and long_sample together name each of the 8 samples exactly once. `long_sample`: see short_sample. `long_rows`: within one bag no row id stands more than 256 times among the first long_len positions, and in every draw some bag has a row id that stands exactly that often. `long_len`: in every draw some long bag has length 500.
All inputs are finite; a program needn't handle non-finite values.
Results may differ from a plain program's by a relative error of at most 0.0003.
Values sent between devices are 32-bit elements; how exact they have to be, the bound alone decides.
No kernel may reach another device: no remote copies, remote signals or barrier semaphores. Data moves between devices by JAX's collectives and lax.ppermute only.
A program may use at most 64 MiB of HBM per device.

v0:
```python
import jax
import jax.numpy as jnp
from jax import lax
from jax.sharding import PartitionSpec as P


def mask_rows(rows, lengths):
    place = lax.broadcasted_iota(jnp.int32, rows.shape, 2)
    return jnp.where(place < lengths[:, :, None], rows, -1)


def pool_rows(keys, table, row_base):
    bag_count = keys.shape[0]
    rows_dev = table.shape[0]
    block = min(8192, rows_dev)
    high_count = block // 128
    local = keys - row_base
    inside = (local >= 0) & (local < rows_dev)
    high = jnp.where(inside, local // 128, -1)
    low = jnp.where(inside, local % 128, -1)
    low_hot = (low[:, :, None] == lax.broadcasted_iota(jnp.int32, (1, 1, 128), 2)).astype(
        jnp.bfloat16
    )

    def add_block(index, total):
        targets = index * high_count + lax.broadcasted_iota(jnp.int32, (1, 1, high_count), 2)
        high_hot = (high[:, :, None] == targets).astype(jnp.bfloat16)
        counts = jnp.einsum("bwh,bwl->bhl", high_hot, low_hot, preferred_element_type=jnp.float32)
        counts = counts.astype(jnp.bfloat16).reshape(bag_count, block)
        piece = lax.dynamic_slice_in_dim(table, index * block, block, 0)
        return total + jnp.dot(counts, piece, preferred_element_type=jnp.float32)

    start = jnp.zeros((bag_count, table.shape[1]), jnp.float32)
    return lax.fori_loop(0, rows_dev // block, add_block, start)


def place_bags(values, lengths, samples, sample_count):
    scaled = values / jnp.sqrt(lengths.astype(jnp.float32))[:, :, None]
    slots = lax.broadcasted_iota(jnp.int32, samples.shape + (sample_count,), 2)
    picks = (samples[:, :, None] == slots).astype(jnp.float32)
    return jnp.sum(picks[:, :, :, None] * scaled[:, :, None, :], axis=0)


def on_device(emb, short_rows, short_len, short_sample, long_rows, long_len, long_sample):
    tab_dev = emb.shape[0]
    short_keys = mask_rows(short_rows, short_len)
    long_keys = mask_rows(long_rows, long_len)
    short_moved, long_moved = (
        lax.all_to_all(short_keys, "table", split_axis=1, concat_axis=0, tiled=True),
        lax.all_to_all(long_keys, "table", split_axis=1, concat_axis=0, tiled=True),
    )
    short_all, long_all = (
        lax.all_gather(short_moved, "batch", axis=0, tiled=True),
        lax.all_gather(long_moved, "batch", axis=0, tiled=True),
    )
    row_base = lax.axis_index("batch") * emb.shape[1]
    short_part = jnp.stack([pool_rows(short_all[:, 0, :], emb[0], row_base)], axis=1)
    long_part = jnp.stack([pool_rows(long_all[:, 0, :], emb[0], row_base)], axis=1)
    short_sum, long_sum = (
        lax.psum_scatter(short_part, "batch", scatter_dimension=0, tiled=True),
        lax.psum_scatter(long_part, "batch", scatter_dimension=0, tiled=True),
    )
    short_back, long_back = (
        lax.all_to_all(short_sum, "table", split_axis=0, concat_axis=1, tiled=True),
        lax.all_to_all(long_sum, "table", split_axis=0, concat_axis=1, tiled=True),
    )
    sample_count = short_sample.shape[0] + long_sample.shape[0]
    pooled = place_bags(short_back, short_len, short_sample, sample_count)
    pooled = pooled + place_bags(long_back, long_len, long_sample, sample_count)
    return jnp.transpose(pooled, (1, 0, 2))


def solution(mesh):
    return jax.shard_map(
        on_device,
        mesh=mesh,
        in_specs=(
            P("table", "batch", None),
            P(("table", "batch"), None, None),
            P(("table", "batch"), None),
            P(("table", "batch"), None),
            P(("table", "batch"), None, None),
            P(("table", "batch"), None),
            P(("table", "batch"), None),
        ),
        out_specs=P(("table", "batch"), None, None),
        check_vma=False,
    )
```

profile of v0, /device:TPU:0, one launch (start us, length us, event | category | flops | bytes accessed | tf_op | source)
XLA Modules:
  0.0 266.0 jit_solution(12417706467865206309)
XLA Ops:
  6.5 0.8 fusion.56
  8.0 4.3 %all-to-all-start = ((s32[4,1,192]{2,1,0:T(1,128)}), s32[4,1,192]{2,1,0:T(1,128)S(1)}, u32[]{:S(2)}, u32[]{:S(2)}) async-start(s32[4,1,192]{2,1,0:T(1,128)} %reshape.94), calls=%async_computation | async-start | bytes 8192 | tf_op jit(solution)/shard_map/all_to_all | solution.py:49
  12.9 0.8 copy.38
  13.8 0.8 copy.42
  15.3 1.4 compare_select_fusion
  17.5 1.3 dynamic-slice
  19.4 3.3 %all-to-all-start.2 = ((s32[2,4,512]{2,0,1:T(2,128)}), s32[2,4,512]{2,0,1:T(2,128)S(1)}, u32[]{:S(2)}, u32[]{:S(2)}) async-start(s32[2,4,512]{2,0,1:T(2,128)} %compare_select_fusion), calls=%async_computation.2 | async-start | bytes 32768 | tf_op jit(solution)/shard_map/all_to_all | solution.py:50
  24.0 31.3 %all_gather.6 = s32[192,1,32]{2,1,0:T(1,128)S(1)} all-gather(s32[24,1,32]{2,1,0:T(1,128)S(1)} %all_to_all.51), channel_id=1, replica_groups=mesh['table'=4,'batch'=8] {'batch'}, dimensions={0}, use_global_device_ids=true | all-gather | bytes 27648 | tf_op jit(solution)/shard_map/all_gather | solution.py:53
  55.4 30.5 %all_gather.7 = s32[64,1,512]{2,0,1:T(8,128)S(1)} all-gather(s32[8,1,512]{2,0,1:T(8,128)S(1)} %all_to_all.58), channel_id=1, replica_groups=mesh['table'=4,'batch'=8] {'batch'}, dimensions={0}, use_global_device_ids=true | all-gather | bytes 147456 | tf_op jit(solution)/shard_map/all_gather | solution.py:54
  86.1 31.9 %while.29 = (s32[]{:T(128)}, f32[64,128]{1,0:T(8,128)S(1)}, s32[64,512]{1,0:T(8,128)S(1)}, bf16[32768,128]{1,0:T(8,128)(2,1)}, s32[64,512]{1,0:T(8,128)S(1)}, /*...) while((s32[]{:T(128)}, f32[64,128]{1,0:T(8,128)S(1)}, s32[64,512]{1,0:T(8,128)S(1)}, ...), condition=%wide.region_5.6_spmd.clone, body=%wide.region_4.5_spmd.clone.sunk | while | flops 682115136 | bytes 4522681 | solution.py:34
  86.1 5.5 %fusion.79 = bf16[64,64,128]{2,1,0:T(8,128)(2,1)S(1)} fusion(s32[64,512]{1,0:T(8,128)S(1)} %get-tuple-element.377, s32[64,512]{1,0:T(8,128)S(1)} %get-tuple-element.375, s32[64]{0:T(128)S(1)} %iota_add_fusion.5), kind=kOutput, calls=%fused_computation.26.clone.1 | convolution fusion | flops 547880960 | bytes 1310976 | tf_op jit(solution)/shard_map/while/body/eval_jaxpr/bwh,bwl->bhl/dot_general | solution.py:28
  91.6 2.4 fusion.80
  94.1 5.5 %fusion.79 = bf16[64,64,128]{2,1,0:T(8,128)(2,1)S(1)} fusion(s32[64,512]{1,0:T(8,128)S(1)} %get-tuple-element.377, s32[64,512]{1,0:T(8,128)S(1)} %get-tuple-element.375, s32[64]{0:T(128)S(1)} %iota_add_fusion.5), kind=kOutput, calls=%fused_computation.26.clone.1 | convolution fusion | flops 547880960 | bytes 1310976 | tf_op jit(solution)/shard_map/while/body/eval_jaxpr/bwh,bwl->bhl/dot_general | solution.py:28
  99.6 2.4 fusion.80
  102.1 5.5 %fusion.79 = bf16[64,64,128]{2,1,0:T(8,128)(2,1)S(1)} fusion(s32[64,512]{1,0:T(8,128)S(1)} %get-tuple-element.377, s32[64,512]{1,0:T(8,128)S(1)} %get-tuple-element.375, s32[64]{0:T(128)S(1)} %iota_add_fusion.5), kind=kOutput, calls=%fused_computation.26.clone.1 | convolution fusion | flops 547880960 | bytes 1310976 | tf_op jit(solution)/shard_map/while/body/eval_jaxpr/bwh,bwl->bhl/dot_general | solution.py:28
  107.6 2.4 fusion.80
  110.1 5.5 %fusion.79 = bf16[64,64,128]{2,1,0:T(8,128)(2,1)S(1)} fusion(s32[64,512]{1,0:T(8,128)S(1)} %get-tuple-element.377, s32[64,512]{1,0:T(8,128)S(1)} %get-tuple-element.375, s32[64]{0:T(128)S(1)} %iota_add_fusion.5), kind=kOutput, calls=%fused_computation.26.clone.1 | convolution fusion | flops 547880960 | bytes 1310976 | tf_op jit(solution)/shard_map/while/body/eval_jaxpr/bwh,bwl->bhl/dot_general | solution.py:28
  115.6 2.4 fusion.80
  118.0 37.0 %all-reduce.1 = f32[64,1,128]{2,0,1:T(8,128)S(1)} all-reduce(f32[64,1,128]{2,0,1:T(8,128)S(1)} %bitcast.97), channel_id=3, replica_groups=mesh['table'=4,'batch'=8] {'batch'}, use_global_device_ids=true, to_apply=%region_6.7.clone | all-reduce | flops 8192 | bytes 65536
  155.7 3.3 %all-to-all-start.3 = ((f32[8,1,128]{2,1,0:T(1,128)}), f32[8,1,128]{2,1,0:T(1,128)S(1)}, u32[]{:S(2)}, u32[]{:S(2)}) async-start(f32[8,1,128]{2,1,0:T(1,128)} %bitcast.13), calls=%async_computation.3 | async-start | bytes 8192 | tf_op jit(solution)/shard_map/all_to_all | solution.py:65
  159.0 35.0 %while.28 = (s32[]{:T(128)}, f32[192,128]{1,0:T(8,128)S(1)}, s32[192,32]{1,0:T(8,128)S(1)}, bf16[32768,128]{1,0:T(8,128)(2,1)}, s32[192,32]{1,0:T(8,128)S(1)}, /...) while((s32[]{:T(128)}, f32[192,128]{1,0:T(8,128)S(1)}, s32[192,32]{1,0:T(8,128)S(1)}, ...), condition=%wide.region_1.2_spmd.clone, body=%wide.region_0.1_spmd.clone.sunk | while | flops 506904640 | bytes 8635065 | solution.py:34
  159.0 5.1 %fusion.73 = bf16[192,64,128]{2,1,0:T(8,128)(2,1)S(1)} fusion(s32[192,32]{1,0:T(8,128)S(1)} %get-tuple-element.347, s32[64]{0:T(128)S(1)} %iota_add_fusion.4, s32[192,32]{1,0:T(8,128)S(1)} %get-tuple-element.345), kind=kOutput, calls=%fused_computation.9.clone.1 | convolution fusion | flops 104202240 | bytes 3195136 | tf_op jit(solution)/shard_map/while/body/eval_jaxpr/bwh,bwl->bhl/dot_general | solution.py:28
  164.1 3.6 %fusion.74 = f32[192,128]{1,0:T(8,128)S(1)} fusion(bf16[32768,128]{1,0:T(8,128)(2,1)} %get-tuple-element.346, s32[]{:T(128)S(6)} %select_n.109, bf16[24,8,64,128]{3,2,1,0:T(8,128)(2,1)S(1)} %bitcast.106, f32[192,128]{1,0:T(8,128)S(1)} %get-tuple-element.334, pred[]{:T(512)S(6)} %compare.18), kind=kOutput, calls=%fused_computation.14.clone.1 | convolution fusion | flops 402702336 | bytes 5439493 | tf_op jit(solution)/shard_map/while/body/eval_jaxpr/dot_general | solution.py:31
  167.7 5.1 %fusion.73 = bf16[192,64,128]{2,1,0:T(8,128)(2,1)S(1)} fusion(s32[192,32]{1,0:T(8,128)S(1)} %get-tuple-element.347, s32[64]{0:T(128)S(1)} %iota_add_fusion.4, s32[192,32]{1,0:T(8,128)S(1)} %get-tuple-element.345), kind=kOutput, calls=%fused_computation.9.clone.1 | convolution fusion | flops 104202240 | bytes 3195136 | tf_op jit(solution)/shard_map/while/body/eval_jaxpr/bwh,bwl->bhl/dot_general | solution.py:28
  172.8 3.6 %fusion.74 = f32[192,128]{1,0:T(8,128)S(1)} fusion(bf16[32768,128]{1,0:T(8,128)(2,1)} %get-tuple-element.346, s32[]{:T(128)S(6)} %select_n.109, bf16[24,8,64,128]{3,2,1,0:T(8,128)(2,1)S(1)} %bitcast.106, f32[192,128]{1,0:T(8,128)S(1)} %get-tuple-element.334, pred[]{:T(512)S(6)} %compare.18), kind=kOutput, calls=%fused_computation.14.clone.1 | convolution fusion | flops 402702336 | bytes 5439493 | tf_op jit(solution)/shard_map/while/body/eval_jaxpr/dot_general | solution.py:31
  176.5 5.1 %fusion.73 = bf16[192,64,128]{2,1,0:T(8,128)(2,1)S(1)} fusion(s32[192,32]{1,0:T(8,128)S(1)} %get-tuple-element.347, s32[64]{0:T(128)S(1)} %iota_add_fusion.4, s32[192,32]{1,0:T(8,128)S(1)} %get-tuple-element.345), kind=kOutput, calls=%fused_computation.9.clone.1 | convolution fusion | flops 104202240 | bytes 3195136 | tf_op jit(solution)/shard_map/while/body/eval_jaxpr/bwh,bwl->bhl/dot_general | solution.py:28
  181.6 3.6 %fusion.74 = f32[192,128]{1,0:T(8,128)S(1)} fusion(bf16[32768,128]{1,0:T(8,128)(2,1)} %get-tuple-element.346, s32[]{:T(128)S(6)} %select_n.109, bf16[24,8,64,128]{3,2,1,0:T(8,128)(2,1)S(1)} %bitcast.106, f32[192,128]{1,0:T(8,128)S(1)} %get-tuple-element.334, pred[]{:T(512)S(6)} %compare.18), kind=kOutput, calls=%fused_computation.14.clone.1 | convolution fusion | flops 402702336 | bytes 5439493 | tf_op jit(solution)/shard_map/while/body/eval_jaxpr/dot_general | solution.py:31
  185.2 5.1 %fusion.73 = bf16[192,64,128]{2,1,0:T(8,128)(2,1)S(1)} fusion(s32[192,32]{1,0:T(8,128)S(1)} %get-tuple-element.347, s32[64]{0:T(128)S(1)} %iota_add_fusion.4, s32[192,32]{1,0:T(8,128)S(1)} %get-tuple-element.345), kind=kOutput, calls=%fused_computation.9.clone.1 | convolution fusion | flops 104202240 | bytes 3195136 | tf_op jit(solution)/shard_map/while/body/eval_jaxpr/bwh,bwl->bhl/dot_general | solution.py:28
  190.3 3.6 %fusion.74 = f32[192,128]{1,0:T(8,128)S(1)} fusion(bf16[32768,128]{1,0:T(8,128)(2,1)} %get-tuple-element.346, s32[]{:T(128)S(6)} %select_n.109, bf16[24,8,64,128]{3,2,1,0:T(8,128)(2,1)S(1)} %bitcast.106, f32[192,128]{1,0:T(8,128)S(1)} %get-tuple-element.334, pred[]{:T(512)S(6)} %compare.18), kind=kOutput, calls=%fused_computation.14.clone.1 | convolution fusion | flops 402702336 | bytes 5439493 | tf_op jit(solution)/shard_map/while/body/eval_jaxpr/dot_general | solution.py:31
  194.7 56.6 %reduce-scatter.6.cloned.1.call-done = f32[24,1,128]{2,0,1:T(8,128)} async-done(((f32[192,1,128]{2,0,1:T(8,128)}), f32[24,1,128]{2,0,1:T(8,128)}) %reduce-scatter.6.cloned.1.call-update) | async-done | bytes 12304
  251.3 3.2 %all-to-all-start.1 = ((f32[24,1,128]{2,1,0:T(1,128)}), f32[24,1,128]{2,1,0:T(1,128)S(1)}, u32[]{:S(2)}, u32[]{:S(2)}) async-start(f32[24,1,128]{2,1,0:T(1,128)} %bitcast.105), calls=%async_computation.1 | async-start | bytes 24576 | tf_op jit(solution)/shard_map/all_to_all | solution.py:64
  254.6 3.7 %all-to-all-done.1 = f32[24,1,128]{2,1,0:T(1,128)S(1)} async-done(((f32[24,1,128]{2,1,0:T(1,128)}), f32[24,1,128]{2,1,0:T(1,128)S(1)}, u32[]{:S(2)}, u32[]{:S(2)}) %all-to-all-start.1) | async-done | bytes 12320 | tf_op jit(solution)/shard_map/all_to_all | solution.py:64
  (41 shorter events, 6.7 us)
Async XLA Ops:
  8.0 11.4 %all-to-all-start = ((s32[4,1,192]{2,1,0:T(1,128)}), s32[4,1,192]{2,1,0:T(1,128)S(1)}, u32[]{:S(2)}, u32[]{:S(2)}) async-start(s32[4,1,192]{2,1,0:T(1,128)} %reshape.94), calls=%async_computation | async-start | bytes 8192 | tf_op jit(solution)/shard_map/all_to_all | solution.py:49
  19.4 36.0 %all-to-all-start.2 = ((s32[2,4,512]{2,0,1:T(2,128)}), s32[2,4,512]{2,0,1:T(2,128)S(1)}, u32[]{:S(2)}, u32[]{:S(2)}) async-start(s32[2,4,512]{2,0,1:T(2,128)} %compare_select_fusion), calls=%async_computation.2 | async-start | bytes 32768 | tf_op jit(solution)/shard_map/all_to_all | solution.py:50
  155.7 39.0 %all-to-all-start.3 = ((f32[8,1,128]{2,1,0:T(1,128)}), f32[8,1,128]{2,1,0:T(1,128)S(1)}, u32[]{:S(2)}, u32[]{:S(2)}) async-start(f32[8,1,128]{2,1,0:T(1,128)} %bitcast.13), calls=%async_computation.3 | async-start | bytes 8192 | tf_op jit(solution)/shard_map/all_to_all | solution.py:65
  158.9 92.3 %reduce-scatter.6.cloned.1.call-start = ((), (), s32[]{:S(2)}) async-start(), calls=%async_computation.5 | async-start | bytes 110592
  194.0 0.6 copy-start
  251.3 7.0 %all-to-all-start.1 = ((f32[24,1,128]{2,1,0:T(1,128)}), f32[24,1,128]{2,1,0:T(1,128)S(1)}, u32[]{:S(2)}, u32[]{:S(2)}) async-start(f32[24,1,128]{2,1,0:T(1,128)} %bitcast.105), calls=%async_computation.1 | async-start | bytes 24576 | tf_op jit(solution)/shard_map/all_to_all | solution.py:64
Sparse Core Ops, SparseCore 0:
  194.7 56.4 reduce-scatter.5
where the time goes:
time: 267 us; the launch traced here: 266 us
  blocking collectives  98.9 us (37%)
  matrix products  66.5 us (25%)
  waiting for transfers between devices  60.3 us (23%)
  starting transfers between devices  14.1 us (5%)
  between operations  14.1 us (5%)
  local copies, waits for them, and re-layouts  6.04 us (2%)
  other arithmetic  5.64 us (2%)
    unnamed x2, waiting for transfers between devices  56.6 us
    dot_general x8, matrix products, add_block(): jnp.einsum('bwh,bwl->bhl', high_hot, low_hot, preferred_element_type=jnp....  42.2 us
    unnamed x1, blocking collectives  37 us
    all_gather x1, blocking collectives, on_device(): lax.all_gather(short_moved, 'batch', axis=0, tiled=True)  31.3 us
    all_gather x1, blocking collectives, on_device(): lax.all_gather(long_moved, 'batch', axis=0, tiled=True)  30.5 us
    dot_general x8, matrix products, add_block(): return total + jnp.dot(counts, piece, preferred_element_type=jnp.float32)  24.3 us
  transfers between devices with their start and end apart: 5, of which 2 were waited for; matrix products, arithmetic and copies ran while one was open for 16% of the time, Pallas kernels for 0%

commit v1 on v0

--- a/solution.py
+++ b/solution.py
@@ -2,6 +2,13 @@
 import jax.numpy as jnp
 from jax import lax
 from jax.sharding import PartitionSpec as P
+
+
+def match_stacks_all(original, axis_name):
+    r_now = lax.axis_size(axis_name)
+    block_now = jnp.stack([original] * r_now, 0)
+    before = lax.all_to_all(block_now, axis_name=axis_name, split_axis=0, concat_axis=0)
+    return jnp.concatenate(before, 0)
 
 
 def mask_rows(rows, lengths):
@@ -50,7 +57,7 @@
         lax.all_to_all(long_keys, "table", split_axis=1, concat_axis=0, tiled=True),
     )
     short_all, long_all = (
-        lax.all_gather(short_moved, "batch", axis=0, tiled=True),
+        match_stacks_all(short_moved, axis_name="batch"),
         lax.all_gather(long_moved, "batch", axis=0, tiled=True),
     )
     row_base = lax.axis_index("batch") * emb.shape[1]

time: 267 us -> 245 us (0.918)
  blocking collectives: 98.9 us -> 68.1 us
  starting transfers between devices: 14.1 us -> 20.3 us
    all_gather x1 -> x0, blocking collectives: 31.3 us -> none  [on_device(): lax.all_gather(short_moved, 'batch', axis=0, tiled=True)]
    all_to_all x0 -> x1, starting transfers between devices: none -> 6.21 us  [match_stacks_all(): lax.all_to_all(block_now, axis_name=axis_name, split_axis=0, concat_axis=0)]
    unnamed x8 -> x11, local copies, waits for them, and re-layouts: 4.75 us -> 5.58 us
  transfers between devices with their start and end apart: 5 -> 6, of which waited for: 2 -> 3; matrix products, arithmetic and copies ran while one was open for 16% -> 31% of each run, Pallas kernels for 0% -> 0%
where the time goes in v1:
time: 245 us
  blocking collectives  68.1 us (28%)
  matrix products  66.3 us (27%)
  waiting for transfers between devices  62.1 us (25%)
  starting transfers between devices  20.3 us (8%)
  between operations  14.2 us (6%)
  local copies, waits for them, and re-layouts  6.86 us (3%)
  other arithmetic  6.28 us (3%)
    unnamed x2, waiting for transfers between devices  56.5 us
    dot_general x8, matrix products, add_block(): jnp.einsum('bwh,bwl->bhl', high_hot, low_hot, preferred_element_type=jnp....  42.2 us
    unnamed x1, blocking collectives  37 us
    all_gather x1, blocking collectives, on_device(): lax.all_gather(long_moved, 'batch', axis=0, tiled=True)  31.1 us
    dot_general x8, matrix products, add_block(): return total + jnp.dot(counts, piece, preferred_element_type=jnp.float32)  24.1 us
    all_to_all x1, starting transfers between devices, match_stacks_all(): lax.all_to_all(block_now, axis_name=axis_name, split_axis=0, concat_axis=0)  6.21 us
    unnamed x11, local copies, waits for them, and re-layouts  5.58 us
  transfers between devices with their start and end apart: 6, of which 3 were waited for; matrix products, arithmetic and copies ran while one was open for 31% of the time, Pallas kernels for 0%

profile of v1, /device:TPU:0, one launch (start us, length us, event | category | flops | bytes accessed | tf_op | source)
XLA Modules:
  0.0 244.6 jit_solution(17174562413746912792)
XLA Ops:
  6.5 0.8 fusion.58
  8.0 4.3 %all-to-all-start = ((s32[4,1,192]{2,1,0:T(1,128)}), s32[4,1,192]{2,1,0:T(1,128)S(1)}, u32[]{:S(2)}, u32[]{:S(2)}) async-start(s32[4,1,192]{2,1,0:T(1,128)} %reshape.99), calls=%async_computation | async-start | bytes 8192 | tf_op jit(solution)/shard_map/all_to_all | solution.py:56
  12.9 0.8 copy.37
  15.3 1.4 compare_select_fusion
  17.5 1.3 dynamic-slice
  19.4 3.3 %all-to-all-start.3 = ((s32[2,4,512]{2,0,1:T(2,128)}), s32[2,4,512]{2,0,1:T(2,128)S(1)}, u32[]{:S(2)}, u32[]{:S(2)}) async-start(s32[2,4,512]{2,0,1:T(2,128)} %compare_select_fusion), calls=%async_computation.3 | async-start | bytes 32768 | tf_op jit(solution)/shard_map/all_to_all | solution.py:57
  24.7 1.9 all-to-all-done.3
  26.6 6.2 %all-to-all-start.1 = ((s32[8,1,768]{2,1,0:T(1,128)}), s32[8,1,768]{2,1,0:T(1,128)S(1)}, u32[]{:S(2)}, u32[]{:S(2)}) async-start(s32[8,1,768]{2,1,0:T(1,128)} %reshape.101), calls=%async_computation.1 | async-start | bytes 49152 | tf_op jit(solution)/shard_map/all_to_all | solution.py:10
  32.8 31.1 %all_gather.3 = s32[64,1,512]{2,0,1:T(8,128)S(1)} all-gather(s32[8,1,512]{2,0,1:T(8,128)S(1)} %all_to_all.59), channel_id=1, replica_groups=mesh['table'=4,'batch'=8] {'batch'}, dimensions={0}, use_global_device_ids=true | all-gather | bytes 147456 | tf_op jit(solution)/shard_map/all_gather | solution.py:61
  64.0 31.7 %while.29 = (s32[]{:T(128)}, f32[64,128]{1,0:T(8,128)S(1)}, s32[64,512]{1,0:T(8,128)S(1)}, bf16[32768,128]{1,0:T(8,128)(2,1)}, s32[64,512]{1,0:T(8,128)S(1)}, /*...) while((s32[]{:T(128)}, f32[64,128]{1,0:T(8,128)S(1)}, s32[64,512]{1,0:T(8,128)S(1)}, ...), condition=%wide.region_5.6_spmd.clone, body=%wide.region_4.5_spmd.clone.sunk | while | flops 682115136 | bytes 4522673 | solution.py:41
  64.0 5.5 %fusion.81 = bf16[64,64,128]{2,1,0:T(8,128)(2,1)S(1)} fusion(s32[64,512]{1,0:T(8,128)S(1)} %get-tuple-element.377, s32[64,512]{1,0:T(8,128)S(1)} %get-tuple-element.375, s32[64]{0:T(128)S(1)} %iota_add_fusion.5), kind=kOutput, calls=%fused_computation.26.clone.1 | convolution fusion | flops 547880960 | bytes 1310976 | tf_op jit(solution)/shard_map/while/body/eval_jaxpr/bwh,bwl->bhl/dot_general | solution.py:35
  69.5 2.4 fusion.82
  72.0 5.5 %fusion.81 = bf16[64,64,128]{2,1,0:T(8,128)(2,1)S(1)} fusion(s32[64,512]{1,0:T(8,128)S(1)} %get-tuple-element.377, s32[64,512]{1,0:T(8,128)S(1)} %get-tuple-element.375, s32[64]{0:T(128)S(1)} %iota_add_fusion.5), kind=kOutput, calls=%fused_computation.26.clone.1 | convolution fusion | flops 547880960 | bytes 1310976 | tf_op jit(solution)/shard_map/while/body/eval_jaxpr/bwh,bwl->bhl/dot_general | solution.py:35
  77.5 2.4 fusion.82
  79.9 5.5 %fusion.81 = bf16[64,64,128]{2,1,0:T(8,128)(2,1)S(1)} fusion(s32[64,512]{1,0:T(8,128)S(1)} %get-tuple-element.377, s32[64,512]{1,0:T(8,128)S(1)} %get-tuple-element.375, s32[64]{0:T(128)S(1)} %iota_add_fusion.5), kind=kOutput, calls=%fused_computation.26.clone.1 | convolution fusion | flops 547880960 | bytes 1310976 | tf_op jit(solution)/shard_map/while/body/eval_jaxpr/bwh,bwl->bhl/dot_general | solution.py:35
  85.4 2.4 fusion.82
  87.8 5.5 %fusion.81 = bf16[64,64,128]{2,1,0:T(8,128)(2,1)S(1)} fusion(s32[64,512]{1,0:T(8,128)S(1)} %get-tuple-element.377, s32[64,512]{1,0:T(8,128)S(1)} %get-tuple-element.375, s32[64]{0:T(128)S(1)} %iota_add_fusion.5), kind=kOutput, calls=%fused_computation.26.clone.1 | convolution fusion | flops 547880960 | bytes 1310976 | tf_op jit(solution)/shard_map/while/body/eval_jaxpr/bwh,bwl->bhl/dot_general | solution.py:35
  93.3 2.4 fusion.82
  95.7 37.0 %all-reduce.1 = f32[64,1,128]{2,0,1:T(8,128)S(1)} all-reduce(f32[64,1,128]{2,0,1:T(8,128)S(1)} %bitcast.134), channel_id=3, replica_groups=mesh['table'=4,'batch'=8] {'batch'}, use_global_device_ids=true, to_apply=%region_6.7.clone | all-reduce | flops 8192 | bytes 65536
  133.4 3.2 %all-to-all-start.4 = ((f32[8,1,128]{2,1,0:T(1,128)}), f32[8,1,128]{2,1,0:T(1,128)S(1)}, u32[]{:S(2)}, u32[]{:S(2)}) async-start(f32[8,1,128]{2,1,0:T(1,128)} %bitcast.13), calls=%async_computation.4 | async-start | bytes 8192 | tf_op jit(solution)/shard_map/all_to_all | solution.py:72
  137.6 35.0 %while.28 = (s32[]{:T(128)}, f32[192,128]{1,0:T(8,128)S(1)}, s32[192,32]{1,0:T(8,128)S(1)}, bf16[32768,128]{1,0:T(8,128)(2,1)}, s32[192,32]{1,0:T(8,128)S(1)}, /...) while((s32[]{:T(128)}, f32[192,128]{1,0:T(8,128)S(1)}, s32[192,32]{1,0:T(8,128)S(1)}, ...), condition=%wide.region_1.2_spmd.clone, body=%wide.region_0.1_spmd.clone.sunk | while | flops 506904640 | bytes 8635057 | solution.py:41
  137.6 5.1 %fusion.75 = bf16[192,64,128]{2,1,0:T(8,128)(2,1)S(1)} fusion(s32[192,32]{1,0:T(8,128)S(1)} %get-tuple-element.347, s32[64]{0:T(128)S(1)} %iota_add_fusion.4, s32[192,32]{1,0:T(8,128)S(1)} %get-tuple-element.345), kind=kOutput, calls=%fused_computation.9.clone.1 | convolution fusion | flops 104202240 | bytes 3195136 | tf_op jit(solution)/shard_map/while/body/eval_jaxpr/bwh,bwl->bhl/dot_general | solution.py:35
  142.7 3.6 %fusion.76 = f32[192,128]{1,0:T(8,128)S(1)} fusion(bf16[32768,128]{1,0:T(8,128)(2,1)} %get-tuple-element.346, s32[]{:T(128)S(6)} %select_n.109, bf16[24,8,64,128]{3,2,1,0:T(8,128)(2,1)S(1)} %bitcast.141, f32[192,128]{1,0:T(8,128)S(1)} %get-tuple-element.334, pred[]{:T(512)S(6)} %compare.18), kind=kOutput, calls=%fused_computation.14.clone.1 | convolution fusion | flops 402702336 | bytes 5439493 | tf_op jit(solution)/shard_map/while/body/eval_jaxpr/dot_general | solution.py:38
  146.3 5.1 %fusion.75 = bf16[192,64,128]{2,1,0:T(8,128)(2,1)S(1)} fusion(s32[192,32]{1,0:T(8,128)S(1)} %get-tuple-element.347, s32[64]{0:T(128)S(1)} %iota_add_fusion.4, s32[192,32]{1,0:T(8,128)S(1)} %get-tuple-element.345), kind=kOutput, calls=%fused_computation.9.clone.1 | convolution fusion | flops 104202240 | bytes 3195136 | tf_op jit(solution)/shard_map/while/body/eval_jaxpr/bwh,bwl->bhl/dot_general | solution.py:35
  151.4 3.6 %fusion.76 = f32[192,128]{1,0:T(8,128)S(1)} fusion(bf16[32768,128]{1,0:T(8,128)(2,1)} %get-tuple-element.346, s32[]{:T(128)S(6)} %select_n.109, bf16[24,8,64,128]{3,2,1,0:T(8,128)(2,1)S(1)} %bitcast.141, f32[192,128]{1,0:T(8,128)S(1)} %get-tuple-element.334, pred[]{:T(512)S(6)} %compare.18), kind=kOutput, calls=%fused_computation.14.clone.1 | convolution fusion | flops 402702336 | bytes 5439493 | tf_op jit(solution)/shard_map/while/body/eval_jaxpr/dot_general | solution.py:38
  155.1 5.1 %fusion.75 = bf16[192,64,128]{2,1,0:T(8,128)(2,1)S(1)} fusion(s32[192,32]{1,0:T(8,128)S(1)} %get-tuple-element.347, s32[64]{0:T(128)S(1)} %iota_add_fusion.4, s32[192,32]{1,0:T(8,128)S(1)} %get-tuple-element.345), kind=kOutput, calls=%fused_computation.9.clone.1 | convolution fusion | flops 104202240 | bytes 3195136 | tf_op jit(solution)/shard_map/while/body/eval_jaxpr/bwh,bwl->bhl/dot_general | solution.py:35
  160.2 3.6 %fusion.76 = f32[192,128]{1,0:T(8,128)S(1)} fusion(bf16[32768,128]{1,0:T(8,128)(2,1)} %get-tuple-element.346, s32[]{:T(128)S(6)} %select_n.109, bf16[24,8,64,128]{3,2,1,0:T(8,128)(2,1)S(1)} %bitcast.141, f32[192,128]{1,0:T(8,128)S(1)} %get-tuple-element.334, pred[]{:T(512)S(6)} %compare.18), kind=kOutput, calls=%fused_computation.14.clone.1 | convolution fusion | flops 402702336 | bytes 5439493 | tf_op jit(solution)/shard_map/while/body/eval_jaxpr/dot_general | solution.py:38
  163.8 5.1 %fusion.75 = bf16[192,64,128]{2,1,0:T(8,128)(2,1)S(1)} fusion(s32[192,32]{1,0:T(8,128)S(1)} %get-tuple-element.347, s32[64]{0:T(128)S(1)} %iota_add_fusion.4, s32[192,32]{1,0:T(8,128)S(1)} %get-tuple-element.345), kind=kOutput, calls=%fused_computation.9.clone.1 | convolution fusion | flops 104202240 | bytes 3195136 | tf_op jit(solution)/shard_map/while/body/eval_jaxpr/bwh,bwl->bhl/dot_general | solution.py:35
  168.9 3.6 %fusion.76 = f32[192,128]{1,0:T(8,128)S(1)} fusion(bf16[32768,128]{1,0:T(8,128)(2,1)} %get-tuple-element.346, s32[]{:T(128)S(6)} %select_n.109, bf16[24,8,64,128]{3,2,1,0:T(8,128)(2,1)S(1)} %bitcast.141, f32[192,128]{1,0:T(8,128)S(1)} %get-tuple-element.334, pred[]{:T(512)S(6)} %compare.18), kind=kOutput, calls=%fused_computation.14.clone.1 | convolution fusion | flops 402702336 | bytes 5439493 | tf_op jit(solution)/shard_map/while/body/eval_jaxpr/dot_general | solution.py:38
  173.3 56.5 %reduce-scatter.6.cloned.1.call-done = f32[24,1,128]{2,0,1:T(8,128)} async-done(((f32[192,1,128]{2,0,1:T(8,128)}), f32[24,1,128]{2,0,1:T(8,128)}) %reduce-scatter.6.cloned.1.call-update) | async-done | bytes 12304
  229.8 3.2 %all-to-all-start.2 = ((f32[24,1,128]{2,1,0:T(1,128)}), f32[24,1,128]{2,1,0:T(1,128)S(1)}, u32[]{:S(2)}, u32[]{:S(2)}) async-start(f32[24,1,128]{2,1,0:T(1,128)} %bitcast.140), calls=%async_computation.2 | async-start | bytes 24576 | tf_op jit(solution)/shard_map/all_to_all | solution.py:71
  233.2 3.7 %all-to-all-done.2 = f32[24,1,128]{2,1,0:T(1,128)S(1)} async-done(((f32[24,1,128]{2,1,0:T(1,128)}), f32[24,1,128]{2,1,0:T(1,128)S(1)}, u32[]{:S(2)}, u32[]{:S(2)}) %all-to-all-start.2) | async-done | bytes 12320 | tf_op jit(solution)/shard_map/all_to_all | solution.py:71
  (46 shorter events, 9.0 us)
Async XLA Ops:
  8.0 11.4 %all-to-all-start = ((s32[4,1,192]{2,1,0:T(1,128)}), s32[4,1,192]{2,1,0:T(1,128)S(1)}, u32[]{:S(2)}, u32[]{:S(2)}) async-start(s32[4,1,192]{2,1,0:T(1,128)} %reshape.99), calls=%async_computation | async-start | bytes 8192 | tf_op jit(solution)/shard_map/all_to_all | solution.py:56
  19.4 7.2 %all-to-all-start.3 = ((s32[2,4,512]{2,0,1:T(2,128)}), s32[2,4,512]{2,0,1:T(2,128)S(1)}, u32[]{:S(2)}, u32[]{:S(2)}) async-start(s32[2,4,512]{2,0,1:T(2,128)} %compare_select_fusion), calls=%async_computation.3 | async-start | bytes 32768 | tf_op jit(solution)/shard_map/all_to_all | solution.py:57
  26.6 106.8 %all-to-all-start.1 = ((s32[8,1,768]{2,1,0:T(1,128)}), s32[8,1,768]{2,1,0:T(1,128)S(1)}, u32[]{:S(2)}, u32[]{:S(2)}) async-start(s32[8,1,768]{2,1,0:T(1,128)} %reshape.101), calls=%async_computation.1 | async-start | bytes 49152 | tf_op jit(solution)/shard_map/all_to_all | solution.py:10
  133.4 39.9 %all-to-all-start.4 = ((f32[8,1,128]{2,1,0:T(1,128)}), f32[8,1,128]{2,1,0:T(1,128)S(1)}, u32[]{:S(2)}, u32[]{:S(2)}) async-start(f32[8,1,128]{2,1,0:T(1,128)} %bitcast.13), calls=%async_computation.4 | async-start | bytes 8192 | tf_op jit(solution)/shard_map/all_to_all | solution.py:72
  136.6 93.2 %reduce-scatter.6.cloned.1.call-start = ((), (), s32[]{:S(2)}) async-start(), calls=%async_computation.6 | async-start | bytes 110592
  172.6 0.6 copy-start
  229.8 7.1 %all-to-all-start.2 = ((f32[24,1,128]{2,1,0:T(1,128)}), f32[24,1,128]{2,1,0:T(1,128)S(1)}, u32[]{:S(2)}, u32[]{:S(2)}) async-start(f32[24,1,128]{2,1,0:T(1,128)} %bitcast.140), calls=%async_computation.2 | async-start | bytes 24576 | tf_op jit(solution)/shard_map/all_to_all | solution.py:71
Sparse Core Ops, SparseCore 0:
  173.4 56.4 reduce-scatter.5
